TPU v7x, 128 devices: a whole 4x4x4 slice. The times are simulated.
128 devices in a mesh: dp: 16 (over x_lo, z, core), tensor: 8 (over y, x_hi).
Axes of the slice: x: 4 (x_hi: 2, x_lo: 2; x = x_hi * 2 + x_lo), y: 4, z: 4, core: 2. Of those that a mesh axis runs over, the one named last changes fastest.
Arguments:
- token_ids: int32 [16, 1024], P('dp', 'tensor'), may hold values from 0 to 30527
- lengths: int32 [16], P('dp'), may hold values from 256 to 1024, as said below
- teacher_bins: int32 [16], P('dp'), may hold values from 0 to 127
- embed_table: bfloat16 [30528, 1024], P('tensor'), may hold values from -6 to 6
- query_key_value_matrix: bfloat16 [1024, 3, 1024], P('dp', None, 'tensor'), may hold values from -2 to 2
- output_matrix: bfloat16 [1024, 1024], P('tensor', 'dp'), may hold values from -0.1875 to 0.1875
- up_matrix: bfloat16 [1024, 4096], P('dp', 'tensor'), may hold values from -0.1875 to 0.1875
- down_matrix: bfloat16 [4096, 1024], P('tensor', 'dp'), may hold values from -0.09375 to 0.09375
- w_head: bfloat16 [1024, 128], P('dp'), may hold values from -64 to 64
Outputs:
- loss: float32 [], replicated
- query_key_value_gradient: float32 [1024, 3, 1024], P('dp', None, 'tensor')
- output_weight_gradient: float32 [1024, 1024], P('tensor', 'dp')
- up_weight_gradient: float32 [1024, 4096], P('dp', 'tensor')
- down_weight_gradient: float32 [4096, 1024], P('tensor', 'dp')
- grad_head: float32 [1024, 128], P('dp')
Inputs may be any that keep to these rules, and one draw needn't show every extreme that they name: lengths[0] is 1024.
All inputs are finite; a program needn't handle non-finite values.
Results may differ from a plain program's by a relative error of at most 0.02.
Values may be sent and summed in bfloat16 or wider, within the bound.
A program may use at most 128 MiB of HBM per device.

v0:
```python
import functools
import types

import jax
import jax.numpy as jnp
from jax import lax
from jax.experimental import pallas as pl
from jax.experimental.pallas import tpu as pltpu
from jax.sharding import Mesh
from jax.sharding import PartitionSpec as P

MESH = pl.DeviceIdType.MESH
EPS = 1e-05
F32 = jnp.float32
BF16 = jnp.bfloat16
HIGH = lax.Precision.HIGHEST
VM = pl.BlockSpec(memory_space=pltpu.VMEM)
SM = pl.BlockSpec(memory_space=pltpu.SMEM)


def where_am_i():
    return {name: lax.axis_index(name) for name in ("xl", "z", "c", "y", "xh")}


def add_mod(value, step, size):
    return lax.rem(value + step, size)


def params(number, mebibytes):
    return pltpu.CompilerParams(
        collective_id=number, has_side_effects=True, vmem_limit_bytes=mebibytes * 2**20
    )


def remote(src, dst, send, recv, device):
    return pltpu.make_async_remote_copy(
        src_ref=src, dst_ref=dst, send_sem=send, recv_sem=recv, device_id=device, device_id_type=MESH
    )


def signal(device):
    pl.semaphore_signal(pltpu.get_barrier_semaphore(), inc=1, device_id=device, device_id_type=MESH)


def normalize(values):
    mean = jnp.mean(values, axis=-1, keepdims=True)
    centered = values - mean
    return centered * lax.rsqrt(jnp.mean(centered * centered, axis=-1, keepdims=True) + EPS)


def normalize_back(values, grad):
    mean = jnp.mean(values, axis=-1, keepdims=True)
    centered = values - mean
    scale = lax.rsqrt(jnp.mean(centered * centered, axis=-1, keepdims=True) + EPS)
    normed = centered * scale
    return scale * (
        grad
        - jnp.mean(grad, axis=-1, keepdims=True)
        - normed * jnp.mean(grad * normed, axis=-1, keepdims=True)
    )


class Ids:
    def __init__(self, src, out, send, recv):
        self.src, self.out, self.send, self.recv = src, out, send, recv
        self.me = where_am_i()
        self.here = self.me["xh"] == self.me["c"]

    def greet(self):
        me = self.me
        for role in range(2):
            for k in range(4):
                source = dict(
                    xl=add_mod(me["xl"], role, 2),
                    c=add_mod(me["xh"], role, 2),
                    xh=me["c"],
                    y=add_mod(me["y"], 4 - k, 4),
                    z=me["z"],
                )
                if role == 0 and k == 0:

                    @pl.when(jnp.logical_not(self.here))
                    def _(source=source):
                        signal(source)
                else:
                    signal(source)
        return jnp.where(self.here, 7, 8)

    def copy(self, role, k):
        me = self.me
        return remote(
            self.src,
            self.out.at[role, me["y"]],
            self.send.at[role, k],
            self.recv.at[role, k],
            dict(
                xl=add_mod(me["xl"], role, 2),
                c=me["xh"],
                xh=add_mod(me["c"], role, 2),
                y=add_mod(me["y"], k, 4),
                z=me["z"],
            ),
        )

    def local(self):
        return pltpu.make_async_copy(self.src, self.out.at[0, self.me["y"]], self.recv.at[0, 0])

    def start(self):
        for role in (1, 0):
            for k in (2, 1, 3, 0):
                if role == 0 and k == 0:

                    @pl.when(jnp.logical_not(self.here))
                    def _():
                        self.copy(0, 0).start()

                    @pl.when(self.here)
                    def _():
                        self.local().start()
                else:
                    self.copy(role, k).start()

    def arrive(self, role):
        for k in range(4):
            place = add_mod(self.me["y"], 4 - k, 4)
            pltpu.make_async_copy(self.src, self.out.at[role, place], self.recv.at[role, k]).wait()

    def sent(self):
        for role in range(2):
            for k in range(4):
                if role == 0 and k == 0:

                    @pl.when(jnp.logical_not(self.here))
                    def _():
                        self.copy(0, 0).wait_send()
                else:
                    self.copy(role, k).wait_send()


class Plane:
    def __init__(self, items, send, recv, collect):
        self.items, self.send, self.recv, self.collect = items, send, recv, collect
        self.me = where_am_i()
        c, xh = self.me["c"], self.me["xh"]
        self.here = xh == c
        self.mine, self.other = (xh, c) if collect else (c, xh)
        self.slot = (self.me["xl"] * 4 + self.me["z"]) * 2 + self.mine
        self.places = [(a, k, e) for k in (2, 1, 3, 0) for a in (1, 0) for e in range(2)]

    def target(self, a, k, e):
        me = self.me
        swapped = dict(c=e, xh=me["c"]) if self.collect else dict(c=me["xh"], xh=e)
        return dict(xl=add_mod(me["xl"], a, 2), z=add_mod(me["z"], k, 4), y=me["y"], **swapped)

    def origin(self, a, k, e):
        me = self.me
        swapped = dict(c=me["xh"], xh=e) if self.collect else dict(c=e, xh=me["c"])
        return dict(xl=add_mod(me["xl"], a, 2), z=add_mod(me["z"], 4 - k, 4), y=me["y"], **swapped)

    def number(self, a, k, e):
        return (add_mod(self.me["xl"], a, 2) * 4 + add_mod(self.me["z"], k, 4)) * 2 + e

    def greet(self):
        for a, k, e in self.places:
            if a == 0 and k == 0:

                @pl.when(jnp.logical_not(jnp.logical_and(self.here, e == self.mine)))
                def _(a=a, k=k, e=e):
                    signal(self.origin(a, k, e))
            else:
                signal(self.origin(a, k, e))
        return jnp.where(self.here, 15, 16)

    def start(self, i):
        block, place = self.items[i][:2]

        def copy(a, k, e):
            return remote(
                block(self.number(a, k, e)), place(self.slot), self.send.at[i], self.recv.at[i], self.target(a, k, e)
            )

        for a, k, e in self.places:
            if a == 0 and k == 0:
                is_self = jnp.logical_and(self.here, e == self.other)

                @pl.when(jnp.logical_not(is_self))
                def _(a=a, k=k, e=e):
                    copy(a, k, e).start()

                @pl.when(is_self)
                def _(a=a, k=k, e=e):
                    pltpu.make_async_copy(
                        block(self.number(a, k, e)), place(self.slot), self.recv.at[i]
                    ).start()
            else:
                copy(a, k, e).start()

    def arrive(self, i):
        whole = self.items[i][2]
        pltpu.make_async_copy(whole, whole, self.recv.at[i]).wait()

    def sent(self, i):
        whole, but_one = self.items[i][2:]

        @pl.when(self.here)
        def _():
            pltpu.make_async_copy(but_one, but_one, self.send.at[i]).wait()

        @pl.when(jnp.logical_not(self.here))
        def _():
            pltpu.make_async_copy(whole, whole, self.send.at[i]).wait()


def rows64(number):
    return pl.ds(pl.multiple_of(number * 64, 64), 64)


def spread_item(shard, target, cols=None):
    cols = pl.ds(0, target.shape[1]) if cols is None else cols
    return (
        lambda number: shard,
        lambda slot: target.at[rows64(slot), cols],
        target.at[:, cols],
        target.at[pl.ds(0, 960), cols],
    )


def collect_item(source, buf):
    return (
        lambda number: source.at[rows64(number)],
        lambda slot: buf.at[slot],
        buf,
        buf.at[pl.ds(0, 15)],
    )


def total_of(buf):
    total = buf[0].astype(F32)
    for s in range(1, 16):
        total = total + buf[s].astype(F32)
    return total


def thirds(row):
    high = row.astype(BF16).astype(F32)
    middle = (row - high).astype(BF16).astype(F32)
    low = row - high - middle
    index = lax.broadcasted_iota(jnp.int32, (8, row.shape[1]), 0)
    rows = jnp.where(index == 0, high, jnp.where(index == 1, middle, jnp.where(index == 2, low, 0.0)))
    return rows.astype(BF16)


def picked(values, start):
    rows = lax.broadcasted_iota(jnp.int32, (64, values.shape[1]), 0)
    cols = lax.broadcasted_iota(jnp.int32, (64, values.shape[1]), 1)
    chosen = (cols == rows + start).astype(F32)
    return lax.dot_general(chosen, values, RHS_T, precision=HIGH, preferred_element_type=F32)


def ring_places():
    me = where_am_i()
    y, c = me["y"], me["c"]
    return me, y, c, add_mod(y, 1, 4), add_mod(y, 3, 4), add_mod(y, 2, 4), 1 - c


class Owner:
    def __init__(self, blocks, stage, far, near, send, recv):
        self.blocks, self.stage, self.far, self.near, self.send, self.recv = blocks, stage, far, near, send, recv
        _, self.y, _, self.up, self.dn, op, _ = ring_places()
        self.first = [
            remote(blocks(op).at[pl.ds(0, 32)], far.at[0], send.at[0], recv.at[0], dict(y=self.up)),
            remote(blocks(op).at[pl.ds(32, 32)], far.at[1], send.at[1], recv.at[1], dict(y=self.dn)),
        ]
        self.second = [
            remote(stage.at[i], near.at[i], send.at[2 + i], recv.at[2 + i], dict(y=(self.up, self.dn)[i]))
            for i in range(2)
        ]

    def begin(self):
        for step in self.first:
            step.start()

    def relay(self):
        blocks, stage, far = self.blocks, self.stage, self.far
        stage[0, 32:64] = blocks(self.up)[32:64]
        stage[1, 0:32] = blocks(self.dn)[0:32]
        self.first[0].wait_recv()
        stage[0, 0:32] = (blocks(self.up)[0:32].astype(F32) + far[0].astype(F32)).astype(BF16)
        self.second[0].start()
        self.first[1].wait_recv()
        stage[1, 32:64] = (blocks(self.dn)[32:64].astype(F32) + far[1].astype(F32)).astype(BF16)
        self.second[1].start()

    def finish(self):
        for step in self.second:
            step.wait_recv()
        return self.blocks(self.y)[...].astype(F32) + self.near[0].astype(F32) + self.near[1].astype(F32)

    def sent(self):
        for step in self.first + self.second:
            step.wait_send()


class Gather:
    def __init__(self, out, chunk, send, recv):
        self.out, self.chunk, self.send, self.recv = out, chunk, send, recv
        _, y, c, up, dn, op, oc = ring_places()
        moves = [
            (y, c, None, dict(y=up)),
            (y, c, None, dict(y=dn)),
            (y, c, None, dict(c=oc)),
            (dn, c, 0, dict(y=up)),
            (dn, c, None, dict(c=oc)),
            (up, c, 1, dict(y=dn)),
            (up, c, None, dict(c=oc)),
            (op, c, 0, dict(c=oc)),
            (op, c, 1, dict(c=oc)),
        ]
        self.steps = []
        for k, (row, col, half, device) in enumerate(moves):
            start = (row * 2 + col) * 128 + chunk * 64
            if half is None:
                ref = out.at[pl.ds(pl.multiple_of(start, 64), 64)]
            else:
                ref = out.at[pl.ds(pl.multiple_of(start + half * 32, 32), 32)]
            self.steps.append(remote(ref, ref, send.at[k], recv.at[k], device))

    def begin(self):
        for k in (0, 1, 2):
            self.steps[k].start()

    def sides(self):
        self.steps[0].wait_recv()
        self.steps[3].start()
        self.steps[4].start()
        self.steps[1].wait_recv()
        self.steps[5].start()
        self.steps[6].start()

    def far(self):
        self.steps[3].wait_recv()
        self.steps[7].start()
        self.steps[5].wait_recv()
        self.steps[8].start()

    def pair_own(self):
        self.steps[2].wait_recv()

    def pair_sides(self):
        self.steps[4].wait_recv()
        self.steps[6].wait_recv()

    def pair_far(self):
        self.steps[7].wait_recv()
        self.steps[8].wait_recv()

    def sent(self):
        for step in self.steps:
            step.wait_send()


def gather_beside(gathers, block_work):
    _, y, c, up, dn, op, oc = ring_places()
    for g in gathers:
        g.pair_own()
    block_work(y)
    for g in gathers:
        g.sides()
    for g in gathers:
        g.pair_sides()
    block_work(up)
    for g in gathers:
        g.far()
    block_work(dn)
    for g in gathers:
        g.pair_far()
    block_work(op)


class PairOwner:
    def __init__(self, terms, r, name):
        self.terms = terms
        get = lambda part: getattr(r, name + part)
        _, y, self.c, self.up, self.dn, self.op, oc = ring_places()
        self.pair, self.summed = get("_pair"), get("_summed")
        self.order = (self.op, self.up, self.dn, y)
        self.steps = [
            remote(
                terms.at[self.rows(b, oc)], self.pair.at[b], get("_psend").at[i], get("_precv").at[i], dict(c=oc)
            )
            for i, b in enumerate(self.order)
        ]
        self.owners = [
            Owner(
                lambda b, ch=ch: self.summed.at[b, pl.ds(ch * 64, 64)],
                get("_stage").at[ch],
                get("_far").at[ch],
                get("_near").at[ch],
                get("_rsend").at[ch],
                get("_rrecv").at[ch],
            )
            for ch in range(2)
        ]

    def rows(self, b, c):
        return pl.ds(pl.multiple_of((b * 2 + c) * 128, 128), 128)

    def push(self, i):
        self.steps[i].start()

    def pull(self, i):
        b = self.order[i]
        self.steps[i].wait_recv()
        self.summed[b] = (self.terms[self.rows(b, self.c)].astype(F32) + self.pair[b].astype(F32)).astype(BF16)

    def sent(self):
        for step in self.steps:
            step.wait_send()
        for owner in self.owners:
            owner.sent()


def pair_owner_scratch(name):
    return {
        name + "_pair": pltpu.VMEM((4, 128, 1024), BF16),
        name + "_summed": pltpu.VMEM((4, 128, 1024), BF16),
        name + "_stage": pltpu.VMEM((2, 2, 64, 1024), BF16),
        name + "_far": pltpu.VMEM((2, 2, 32, 1024), BF16),
        name + "_near": pltpu.VMEM((2, 2, 64, 1024), BF16),
        name + "_psend": pltpu.SemaphoreType.DMA((4,)),
        name + "_precv": pltpu.SemaphoreType.DMA((4,)),
        name + "_rsend": pltpu.SemaphoreType.DMA((2, 4)),
        name + "_rrecv": pltpu.SemaphoreType.DMA((2, 4)),
        name + "_asend": pltpu.SemaphoreType.DMA((2, 9)),
        name + "_arecv": pltpu.SemaphoreType.DMA((2, 9)),
    }


SCALE = 0.125
PACKET = 512 + 1024 + 1024 + 128 + 128
LHS_T = (((0,), (0,)), ((), ()))
RHS_T = (((1,), (1,)), ((), ()))


def rows256(b):
    return pl.ds(pl.multiple_of(b * 256, 256), 256)


def of_head(value, head, axis):
    index = lax.broadcasted_iota(jnp.int32, value.shape, axis)
    return jnp.where((index >= 64) == (head == 1), value, jnp.zeros_like(value))


def step_kernel(names, *refs):
    r = types.SimpleNamespace(**dict(zip(names, refs, strict=True)))
    me, y, c, up, dn, op, oc = ring_places()
    slot = y * 2 + c
    vocab, padded = r.table.shape[0], r.shard.shape[0]

    fetch = pltpu.make_async_copy(r.table, r.shard.at[pl.ds(0, vocab)], r.load.at[0])
    fetch_ids = pltpu.make_async_copy(r.ids, r.ids_here, r.load.at[1])
    fetch_ids.start()
    fetch.start()
    tokens = Ids(r.packet_in, r.got, r.isend, r.irecv)
    spread = Plane(
        [spread_item(r.qkv_s.at[i], r.qkv_w, pl.ds(i * 128, 128)) for i in range(3)]
        + [
            spread_item(r.out_s, r.out_w),
            spread_item(r.up_s, r.up_w),
            spread_item(r.head_s, r.head_w),
            spread_item(r.down_s, r.down_w),
        ],
        r.ssend,
        r.srecv,
        False,
    )
    collect = Plane(
        [
            (lambda number: r.packet, lambda slot: r.packets.at[slot], r.packets, r.packets.at[pl.ds(0, 15)]),
            collect_item(r.up_term, r.up_buf),
            collect_item(r.out_term, r.out_buf),
        ]
        + [collect_item(r.qkv_term.at[i], r.qkv_buf.at[i]) for i in range(3)],
        r.csend,
        r.crecv,
        True,
    )
    partner = dict(xl=1 - me["xl"], xh=1 - me["xh"])
    peers = [(k, e) for k in (2, 1, 3, 0) for e in range(2) if (k, e) != (0, 0)]
    for device in (dict(y=up), dict(y=dn), dict(c=oc), partner):
        signal(device)
    for k, e in peers:
        signal(dict(y=add_mod(y, (4 - k) % 4, 4), c=add_mod(c, e, 2)))
    greeted = tokens.greet() + spread.greet() + collect.greet() + 11
    if padded > vocab:
        r.shard[vocab:padded] = jnp.zeros((padded - vocab, 1024), BF16)
    fetch_ids.wait()
    line = lax.broadcasted_iota(jnp.int32, (8, 128), 0)
    r.packet_in[...] = jnp.where(line == 0, r.ids_here[...], jnp.where(line == 1, r.count[0], r.label[0]))
    pl.semaphore_wait(pltpu.get_barrier_semaphore(), greeted)
    tokens.start()
    for i in range(4):
        spread.start(i)

    base = (y * 2 + me["xh"]) * vocab
    lanes = lax.broadcasted_iota(jnp.int32, (64, 128), 1)

    def look_up(role, ch):
        for b in range(4):
            wanted = jnp.broadcast_to(r.got[role, b, 0:1, :], (128, 128)).T[ch * 64 : ch * 64 + 64] - base
            for tile in range(padded // 128):
                r.chosen[b * 64 : b * 64 + 64, tile * 128 : tile * 128 + 128] = jnp.where(
                    wanted == lanes + tile * 128, 1.0, 0.0
                ).astype(BF16)
        if role == 1 and ch == 0:
            fetch.wait()
        for part in range(4):
            cols = slice(part * 256, part * 256 + 256)
            found = jnp.dot(r.chosen[...], r.shard[:, cols], preferred_element_type=F32).astype(BF16)
            for b in range(4):
                r.rows[role, ch, b, :, cols] = found[b * 64 : b * 64 + 64]

    own = {
        (role, ch): Owner(
            lambda b, role=role, ch=ch: r.rows.at[role, ch, b],
            r.e_stage.at[role, ch],
            r.e_far.at[role, ch],
            r.e_near.at[role, ch],
            r.e_rsend.at[role, ch],
            r.e_rrecv.at[role, ch],
        )
        for role in range(2)
        for ch in range(2)
    }
    cross = [
        remote(r.total.at[ch], r.theirs.at[ch], r.xsend.at[ch], r.xrecv.at[ch], partner) for ch in range(2)
    ]
    tokens.arrive(1)
    look_up(1, 0)
    own[1, 0].begin()
    look_up(1, 1)
    own[1, 1].begin()
    own[1, 0].relay()
    tokens.arrive(0)
    look_up(0, 0)
    own[0, 0].begin()
    own[1, 1].relay()
    r.total[0] = own[1, 0].finish().astype(BF16)
    cross[0].start()
    look_up(0, 1)
    own[0, 1].begin()
    own[0, 0].relay()
    r.total[1] = own[1, 1].finish().astype(BF16)
    cross[1].start()
    for i in range(4, 7):
        spread.start(i)
    own[0, 1].relay()
    length, label = r.got[0, 0, 1:2, 0:1], r.got[0, 0, 2:3, 0:1]
    gathers = [Gather(r.normed, ch, r.e_asend.at[ch], r.e_arecv.at[ch]) for ch in range(2)]
    first = []

    def own_rows(ch):
        return pl.ds(pl.multiple_of(slot * 128 + ch * 64, 64), 64)

    for ch in range(2):
        mine = own[0, ch].finish()
        cross[ch].wait_recv()
        value = mine + r.theirs[ch].astype(F32)
        first.append(value)
        r.normed[own_rows(ch)] = normalize(value).astype(BF16)
        gathers[ch].begin()
    for ch in range(2):
        r.first[ch * 64 : ch * 64 + 64] = first[ch]
    for i in range(4):
        spread.arrive(i)

    def project(b):
        r.qkv[rows256(b)] = jnp.dot(r.normed[rows256(b)], r.qkv_w[...], preferred_element_type=F32).astype(BF16)

    gather_beside(gathers, project)

    r.query_t[...] = (r.qkv[:, 0:128] * SCALE).T
    r.values_t[...] = r.qkv[:, 256:384].T
    r.out_t[...] = r.out_w[...].T
    seen = lax.broadcasted_iota(jnp.int32, (1024, 256), 0) < length

    def attend(b):
        cols = rows256(b)
        for head in range(2):
            scores = jnp.dot(
                r.qkv[:, 128:256], of_head(r.query_t[:, cols], head, 0), preferred_element_type=F32
            )
            scores = jnp.where(seen, scores, -1e30)
            expo = jnp.exp(scores - jnp.max(scores, axis=0, keepdims=True))
            probs = (expo * (1.0 / jnp.sum(expo, axis=0, keepdims=True))).astype(BF16)
            r.probs_t[head, :, cols] = probs
            rows = slice(head * 64, head * 64 + 64)
            r.context_t[rows, cols] = jnp.dot(
                r.values_t[rows], probs, preferred_element_type=F32
            ).astype(BF16)
        r.terms[cols] = jnp.dot(r.context_t[:, cols].T, r.out_t[...], preferred_element_type=F32).astype(BF16)

    summed = PairOwner(r.terms, r, "a")
    attend(op)
    summed.push(0)
    attend(up)
    summed.push(1)
    summed.pull(0)
    for owner in summed.owners:
        owner.begin()
    attend(dn)
    summed.push(2)
    summed.pull(1)
    attend(y)
    summed.push(3)
    summed.pull(2)
    for owner in summed.owners:
        owner.relay()
    summed.pull(3)
    more = [Gather(r.normed_two, ch, r.a_asend.at[ch], r.a_arecv.at[ch]) for ch in range(2)]
    for ch in range(2):
        second = (r.first[ch * 64 : ch * 64 + 64] + summed.owners[ch].finish()).astype(BF16)
        r.second[ch * 64 : ch * 64 + 64] = second
        r.normed_two[own_rows(ch)] = normalize(second.astype(F32)).astype(BF16)
        more[ch].begin()

    def live(start, size):
        return start + lax.broadcasted_iota(jnp.int32, (size, 1), 0) < length

    r.hidden_sum[...] = jnp.zeros((1, 512), F32)
    spread.arrive(4)

    def hidden_block(b):
        hidden = jnp.dot(r.normed_two[rows256(b)], r.up_w[...], preferred_element_type=F32)
        square = hidden * hidden
        inner = jnp.tanh(0.7978845608028654 * hidden * (1.0 + 0.044715 * square))
        half = 0.5 * (1.0 + inner)
        acted = (hidden * half).astype(BF16).astype(F32)
        r.slope[rows256(b)] = half + 0.5 * hidden * (1.0 - inner * inner) * (
            0.7978845608028654 + (0.7978845608028654 * 3.0 * 0.044715) * square
        )
        r.hidden_sum[...] += jnp.sum(jnp.where(live(b * 256, 256), acted, 0.0), axis=0, keepdims=True)

    gather_beside(more, hidden_block)

    spread.arrive(5)
    spread.arrive(6)
    hidden_sum = r.hidden_sum[...]
    own_sum = jnp.sum(jnp.where(live(slot * 128, 128), r.second[...].astype(F32), 0.0), axis=0, keepdims=True)
    pushed = lax.dot_general(thirds(hidden_sum), r.down_w[...], RHS_T, preferred_element_type=F32)
    r.parts[slot] = own_sum + jnp.sum(pushed, axis=0, keepdims=True)
    small = [
        remote(
            r.parts.at[slot],
            r.parts.at[slot],
            r.hsend.at[k, e],
            r.hrecv.at[k, e],
            dict(y=add_mod(y, k, 4), c=add_mod(c, e, 2)),
        )
        for k, e in peers
    ]
    for step in small:
        step.start()
    for step in small:
        step.wait()
    pooled = r.parts[0]
    for s in range(1, 8):
        pooled = pooled + r.parts[s]
    count = length.astype(F32)
    pooled = pooled / count
    final = normalize(pooled)
    logits = jnp.sum(jnp.dot(thirds(final), r.head_w[...], preferred_element_type=F32), axis=0, keepdims=True)
    top = jnp.max(logits, axis=-1, keepdims=True)
    total = jnp.log(jnp.sum(jnp.exp(logits - top), axis=-1, keepdims=True)) + top
    labels = (lax.broadcasted_iota(jnp.int32, logits.shape, 1) == label).astype(F32)
    loss = total - jnp.sum(logits * labels, axis=-1, keepdims=True)
    g_logits = (jnp.exp(logits - total) - labels) / 16.0
    g_final = lax.dot_general(thirds(g_logits), r.head_w[...], RHS_T, preferred_element_type=F32)
    per_token = normalize_back(pooled, jnp.sum(g_final, axis=0, keepdims=True)) / count
    rounded = per_token.astype(BF16)
    pulled = jnp.dot(rounded, r.down_w[...], preferred_element_type=F32)

    back = PairOwner(r.terms_back, r, "b")
    for i, b in enumerate(back.order):
        rows = rows256(b)
        grad = jnp.where(live(b * 256, 256), r.slope[rows] * pulled, 0.0).astype(BF16)
        r.g_pre[rows] = grad
        r.terms_back[rows] = lax.dot_general(
            grad, r.up_w[...], RHS_T, preferred_element_type=F32
        ).astype(BF16)
        back.push(i)
    back.pull(0)
    for owner in back.owners:
        owner.begin()
    for i in range(1, 4):
        back.pull(i)
    for block in range(4):
        cols = pl.ds(block * 256, 256)
        r.up_term[cols] = lax.dot_general(
            r.normed_two[:, cols], r.g_pre[...], LHS_T, preferred_element_type=F32
        ).astype(BF16)
    for owner in back.owners:
        owner.relay()
    r.packet[:, 0:512] = hidden_sum
    r.packet[:, 512:1536] = rounded.astype(F32)
    r.packet[:, 1536:2560] = final
    r.packet[:, 2560:2688] = g_logits
    r.packet[:, 2688:2816] = jnp.broadcast_to(loss, (1, 128))
    collect.start(1)
    collect.start(0)
    last = [Gather(r.g_second, ch, r.b_asend.at[ch], r.b_arecv.at[ch]) for ch in range(2)]
    for ch in range(2):
        grad = normalize_back(r.second[ch * 64 : ch * 64 + 64].astype(F32), back.owners[ch].finish())
        grad += jnp.where(live(slot * 128 + ch * 64, 64), per_token, 0.0)
        r.g_second[own_rows(ch)] = grad.astype(BF16)
        last[ch].begin()

    r.keys_t[...] = (r.qkv[:, 128:256] * SCALE).T
    r.grad_k[...] = jnp.zeros((1024, 128), F32)
    r.grad_v[...] = jnp.zeros((1024, 128), F32)

    def attend_back(b):
        cols = rows256(b)
        g_context = jnp.dot(r.g_second[cols], r.out_w[...], preferred_element_type=F32)
        g_context_t = g_context.T
        g_context = g_context.astype(BF16)
        product = g_context_t * r.context_t[:, cols].astype(F32)
        query = r.qkv[cols, 0:128] * SCALE
        for head in range(2):
            rows = slice(head * 64, head * 64 + 64)
            probs = r.probs_t[head, :, cols]
            delta = jnp.sum(product[rows], axis=0, keepdims=True)
            moved = jnp.dot(
                r.qkv[:, 256:384], of_head(g_context_t, head, 0).astype(BF16), preferred_element_type=F32
            )
            g_scores = (probs.astype(F32) * (moved - delta)).astype(BF16)
            r.grad_q[rows, cols] = jnp.dot(
                r.keys_t[rows], g_scores, preferred_element_type=F32
            ).astype(BF16)
            r.grad_k[...] += jnp.dot(g_scores, of_head(query, head, 1), preferred_element_type=F32)
            r.grad_v[...] += jnp.dot(probs, of_head(g_context, head, 1), preferred_element_type=F32)

    gather_beside(last, attend_back)
    r.out_term[...] = jnp.dot(r.context_t[...], r.g_second[...], preferred_element_type=F32).T.astype(BF16)
    collect.start(2)
    for piece in range(3):
        left = r.grad_q[...] if piece == 0 else (r.grad_k, r.grad_v)[piece - 1][...].T.astype(BF16)
        r.qkv_term[piece] = jnp.dot(left, r.normed[...], preferred_element_type=F32).T.astype(BF16)
        collect.start(3 + piece)

    collect.arrive(0)
    begin = ((me["xl"] * 4 + me["z"]) * 2 + me["c"]) * 64
    packets = jnp.concatenate([r.packets[s] for s in range(16)], axis=0)
    r.down_grad[...] = jnp.dot(
        picked(packets[:, 512:1536], begin), packets[:, 0:512], precision=HIGH, preferred_element_type=F32
    )
    r.head_grad[...] = jnp.dot(
        picked(packets[:, 1536:2560], begin), packets[:, 2560:2688], precision=HIGH, preferred_element_type=F32
    )
    r.loss[...] = jnp.sum(packets[:, 2688:2816], axis=0, keepdims=True) / 16.0
    collect.arrive(1)
    r.up_grad[...] = total_of(r.up_buf)

    tokens.sent()
    for i in range(7):
        spread.sent(i)
    for owner in own.values():
        owner.sent()
    for step in cross:
        step.wait_send()
    for g in gathers + more + last:
        g.sent()
    summed.sent()
    back.sent()
    for i in range(6):
        collect.sent(i)
    for i in range(2, 6):
        collect.arrive(i)


HBM = pl.BlockSpec(memory_space=pltpu.HBM)


def step(count, label, ids, table, qkv_s, out_s, up_s, down_s, head_s):
    padded = -(-table.shape[0] // 256) * 256
    inputs = dict(
        count=SM, label=SM, ids=HBM, table=HBM, qkv_s=HBM, out_s=HBM, up_s=HBM, down_s=HBM, head_s=HBM
    )
    outputs = dict(
        up_grad=jax.ShapeDtypeStruct((64, 512), F32),
        down_grad=jax.ShapeDtypeStruct((64, 512), F32),
        head_grad=jax.ShapeDtypeStruct((64, 128), F32),
        loss=jax.ShapeDtypeStruct((1, 128), F32),
        out_buf=jax.ShapeDtypeStruct((16, 64, 128), BF16),
        qkv_buf=jax.ShapeDtypeStruct((3, 16, 64, 128), BF16),
    )
    dma = pltpu.SemaphoreType.DMA
    vm = pltpu.VMEM
    scratch = dict(
        load=dma((2,)),
        ids_here=vm((1, 128), jnp.int32),
        packet_in=vm((8, 128), jnp.int32),
        got=vm((2, 4, 8, 128), jnp.int32),
        isend=dma((2, 4)),
        irecv=dma((2, 4)),
        ssend=dma((7,)),
        srecv=dma((7,)),
        csend=dma((6,)),
        crecv=dma((6,)),
        shard=vm((padded, 1024), BF16),
        chosen=vm((256, padded), BF16),
        rows=vm((2, 2, 4, 64, 1024), BF16),
        e_stage=vm((2, 2, 2, 64, 1024), BF16),
        e_far=vm((2, 2, 2, 32, 1024), BF16),
        e_near=vm((2, 2, 2, 64, 1024), BF16),
        e_rsend=dma((2, 2, 4)),
        e_rrecv=dma((2, 2, 4)),
        e_asend=dma((2, 9)),
        e_arecv=dma((2, 9)),
        total=vm((2, 64, 1024), BF16),
        theirs=vm((2, 64, 1024), BF16),
        xsend=dma((2,)),
        xrecv=dma((2,)),
        first=vm((128, 1024), F32),
        normed=vm((1024, 1024), BF16),
        qkv_w=vm((1024, 384), BF16),
        out_w=vm((1024, 128), BF16),
        up_w=vm((1024, 512), BF16),
        down_w=vm((1024, 512), BF16),
        head_w=vm((1024, 128), BF16),
        qkv=vm((1024, 384), BF16),
        query_t=vm((128, 1024), BF16),
        values_t=vm((128, 1024), BF16),
        keys_t=vm((128, 1024), BF16),
        out_t=vm((128, 1024), BF16),
        probs_t=vm((2, 1024, 1024), BF16),
        context_t=vm((128, 1024), BF16),
        terms=vm((1024, 1024), BF16),
        **pair_owner_scratch("a"),
        second=vm((128, 1024), BF16),
        normed_two=vm((1024, 1024), BF16),
        hidden_sum=vm((1, 512), F32),
        slope=vm((1024, 512), F32),
        parts=vm((8, 1, 1024), F32),
        hsend=dma((4, 2)),
        hrecv=dma((4, 2)),
        g_pre=vm((1024, 512), BF16),
        terms_back=vm((1024, 1024), BF16),
        **pair_owner_scratch("b"),
        up_term=vm((1024, 512), BF16),
        up_buf=vm((16, 64, 512), BF16),
        packet=vm((1, PACKET), F32),
        packets=vm((16, 1, PACKET), F32),
        g_second=vm((1024, 1024), BF16),
        grad_q=vm((128, 1024), BF16),
        grad_k=vm((1024, 128), F32),
        grad_v=vm((1024, 128), F32),
        out_term=vm((1024, 128), BF16),
        qkv_term=vm((3, 1024, 128), BF16),
    )
    return pl.pallas_call(
        functools.partial(step_kernel, (*inputs, *outputs, *scratch)),
        out_shape=list(outputs.values()),
        in_specs=list(inputs.values()),
        out_specs=[VM] * len(outputs),
        scratch_shapes=list(scratch.values()),
        compiler_params=params(1, 61),
        name="step",
    )(count, label, ids, table, qkv_s, out_s, up_s, down_s, head_s)


def results_kernel(up, down, head, out_buf, qkv_buf, up_grad, down_grad, head_grad, out_grad, qkv_grad):
    up_grad[...] = up[...]
    down_grad[...] = down[...]
    head_grad[...] = head[...]
    out_grad[...] = total_of(out_buf)
    for i in range(3):
        qkv_grad[i] = total_of(qkv_buf.at[i])


def results(*arrays):
    return pl.pallas_call(
        results_kernel,
        out_shape=[
            jax.ShapeDtypeStruct((64, 512), F32),
            jax.ShapeDtypeStruct((64, 512), F32),
            jax.ShapeDtypeStruct((64, 128), F32),
            jax.ShapeDtypeStruct((64, 128), F32),
            jax.ShapeDtypeStruct((3, 64, 128), F32),
        ],
        in_specs=[VM] * 5,
        out_specs=[VM] * 5,
        compiler_params=pltpu.CompilerParams(vmem_limit_bytes=8 * 2**20),
        name="results",
    )(*arrays)


def per_device(token_ids, lengths, teacher_bins, table, qkv_shard, out_shard, up_shard, down_shard, head_shard):
    up_grad, down_grad, head_grad, loss, out_buf, qkv_buf = step(
        lengths,
        teacher_bins,
        token_ids,
        table,
        jnp.transpose(qkv_shard, (1, 0, 2)),
        out_shard.T,
        up_shard,
        down_shard.T,
        head_shard,
    )
    up_grad, down_grad, head_grad, out_grad, qkv_grad = results(up_grad, down_grad, head_grad, out_buf, qkv_buf)
    return loss[0, 0], jnp.transpose(qkv_grad, (1, 0, 2)), out_grad.T, up_grad, down_grad.T, head_grad


def solution(mesh):
    fine = Mesh(mesh.devices.reshape(2, 4, 2, 4, 2), ("xl", "z", "c", "y", "xh"))
    dp, tensor = ("xl", "z", "c"), ("y", "xh")
    return jax.shard_map(
        per_device,
        mesh=fine,
        in_specs=(
            P(dp, tensor),
            P(dp),
            P(dp),
            P(tensor, None),
            P(dp, None, tensor),
            P(tensor, dp),
            P(dp, tensor),
            P(tensor, dp),
            P(dp, None),
        ),
        out_specs=(
            P(),
            P(dp, None, tensor),
            P(tensor, dp),
            P(dp, tensor),
            P(tensor, dp),
            P(dp, None),
        ),
        check_vma=False,
    )
```

profile of v0, /device:TPU:1, one launch (start us, length us, event | category | flops | bytes accessed | tf_op | source)
XLA Modules:
  0.0 136.9 jit_solution(3762670179533022387)
XLA Ops:
  1.9 127.7 %step.1 = (f32[64,512]{1,0:T(8,128)}, f32[64,512]{1,0:T(8,128)}, f32[64,128]{1,0:T(8,128)}, f32[1,128]{1,0:T(1,128)}, bf16[16,64,128]{2,1,0:T(8,128)(2,1)}, /*index=5*/bf16[3,16,64,128]{3,2,1,0:T(8,128)(2,1)}) custom-call(s32[1]{0:T(128)S(6)} %copy.16.refs_0_, s32[1]{0:T(128)S(6)} %copy.17.refs_1_, s32[1,128]{1,0:T(1,128)} %refs_2_.1, ...), custom_call_target="tpu_custom_call" | custom-call | tf_op jit(solution)/shard_map/step/pallas_call | solution.py:861
  129.6 0.0 copy-start
  129.6 1.1 copy-done
  130.8 0.0 copy-start.1
  130.8 0.9 copy-done.1
  131.7 0.0 copy-start.2
  131.7 0.9 copy-done.2
  132.6 0.0 copy-start.3
  132.6 0.9 copy-done.3
  133.5 0.0 copy-start.4
  133.5 0.8 copy-done.4
  134.3 0.8 results.1
Async XLA Ops:
  129.6 1.1 copy-start
  130.8 0.9 copy-start.1
  131.7 0.9 copy-start.2
  132.6 0.9 copy-start.3
  133.5 0.8 copy-start.4
where the time goes:
time: 137 us
  Pallas kernels  129 us (94%)
  local copies, waits for them, and re-layouts  4.64 us (3%)
  between operations  3.71 us (3%)
    pallas_call x1, Pallas kernels, step(): pl.pallas_call(functools.partial(step_kernel, (*inputs, *outputs, *scratc...  128 us
    unnamed x10, local copies, waits for them, and re-layouts  4.64 us

commit v1 on v0

--- a/solution.py
+++ b/solution.py
@@ -265,39 +265,43 @@
 
 class Owner:
     def __init__(self, blocks, stage, far, near, send, recv):
-        self.blocks, self.stage, self.far, self.near, self.send, self.recv = blocks, stage, far, near, send, recv
+        self.blocks, self.stage, self.far, self.near = blocks, stage, far, near
         _, self.y, _, self.up, self.dn, op, _ = ring_places()
-        self.first = [
-            remote(blocks(op).at[pl.ds(0, 32)], far.at[0], send.at[0], recv.at[0], dict(y=self.up)),
-            remote(blocks(op).at[pl.ds(32, 32)], far.at[1], send.at[1], recv.at[1], dict(y=self.dn)),
-        ]
+        self.ways = (self.up, self.dn)
+        self.parts = (pl.ds(0, 32), pl.ds(32, 32))
+
+        def go(k, source, target, side):
+            return remote(source, target, send.at[k], recv.at[k], dict(y=self.ways[side]))
+
+        self.first = [go(i, blocks(op).at[self.parts[i]], far.at[i], i) for i in range(2)]
         self.second = [
-            remote(stage.at[i], near.at[i], send.at[2 + i], recv.at[2 + i], dict(y=(self.up, self.dn)[i]))
+            go(2 + i, blocks(self.ways[i]).at[self.parts[1 - i]], near.at[i, self.parts[1 - i]], i)
             for i in range(2)
         ]
+        self.third = [go(4 + i, stage.at[i], near.at[i, self.parts[i]], i) for i in range(2)]
 
     def begin(self):
         for step in self.first:
             step.start()
 
+    def early(self, sides=(0, 1)):
+        for i in sides:
+            self.second[i].start()
+
     def relay(self):
-        blocks, stage, far = self.blocks, self.stage, self.far
-        stage[0, 32:64] = blocks(self.up)[32:64]
-        stage[1, 0:32] = blocks(self.dn)[0:32]
-        self.first[0].wait_recv()
-        stage[0, 0:32] = (blocks(self.up)[0:32].astype(F32) + far[0].astype(F32)).astype(BF16)
-        self.second[0].start()
-        self.first[1].wait_recv()
-        stage[1, 32:64] = (blocks(self.dn)[32:64].astype(F32) + far[1].astype(F32)).astype(BF16)
-        self.second[1].start()
+        for i in range(2):
+            self.first[i].wait_recv()
+            mine = self.blocks(self.ways[i])[self.parts[i]]
+            self.stage[i] = (mine.astype(F32) + self.far[i].astype(F32)).astype(BF16)
+            self.third[i].start()
 
     def finish(self):
-        for step in self.second:
+        for step in self.second + self.third:
             step.wait_recv()
         return self.blocks(self.y)[...].astype(F32) + self.near[0].astype(F32) + self.near[1].astype(F32)
 
     def sent(self):
-        for step in self.first + self.second:
+        for step in self.first + self.second + self.third:
             step.wait_send()
 
 
@@ -359,7 +363,7 @@
             step.wait_send()
 
 
-def gather_beside(gathers, block_work):
+def gather_beside(gathers, block_work, last_work=None):
     _, y, c, up, dn, op, oc = ring_places()
     for g in gathers:
         g.pair_own()
@@ -374,7 +378,7 @@
     block_work(dn)
     for g in gathers:
         g.pair_far()
-    block_work(op)
+    (last_work or block_work)(op)
 
 
 class PairOwner:
@@ -424,13 +428,13 @@
     return {
         name + "_pair": pltpu.VMEM((4, 128, 1024), BF16),
         name + "_summed": pltpu.VMEM((4, 128, 1024), BF16),
-        name + "_stage": pltpu.VMEM((2, 2, 64, 1024), BF16),
+        name + "_stage": pltpu.VMEM((2, 2, 32, 1024), BF16),
         name + "_far": pltpu.VMEM((2, 2, 32, 1024), BF16),
         name + "_near": pltpu.VMEM((2, 2, 64, 1024), BF16),
         name + "_psend": pltpu.SemaphoreType.DMA((4,)),
         name + "_precv": pltpu.SemaphoreType.DMA((4,)),
-        name + "_rsend": pltpu.SemaphoreType.DMA((2, 4)),
-        name + "_rrecv": pltpu.SemaphoreType.DMA((2, 4)),
+        name + "_rsend": pltpu.SemaphoreType.DMA((2, 6)),
+        name + "_rrecv": pltpu.SemaphoreType.DMA((2, 6)),
         name + "_asend": pltpu.SemaphoreType.DMA((2, 9)),
         name + "_arecv": pltpu.SemaphoreType.DMA((2, 9)),
     }
@@ -499,7 +503,7 @@
     r.packet_in[...] = jnp.where(line == 0, r.ids_here[...], jnp.where(line == 1, r.count[0], r.label[0]))
     pl.semaphore_wait(pltpu.get_barrier_semaphore(), greeted)
     tokens.start()
-    for i in range(4):
+    for i in range(3):
         spread.start(i)
 
     base = (y * 2 + me["xh"]) * vocab
@@ -538,21 +542,25 @@
     tokens.arrive(1)
     look_up(1, 0)
     own[1, 0].begin()
+    own[1, 0].early()
     look_up(1, 1)
     own[1, 1].begin()
+    own[1, 1].early()
     own[1, 0].relay()
     tokens.arrive(0)
     look_up(0, 0)
     own[0, 0].begin()
+    own[0, 0].early()
     own[1, 1].relay()
     r.total[0] = own[1, 0].finish().astype(BF16)
     cross[0].start()
     look_up(0, 1)
     own[0, 1].begin()
+    own[0, 1].early()
     own[0, 0].relay()
     r.total[1] = own[1, 1].finish().astype(BF16)
     cross[1].start()
-    for i in range(4, 7):
+    for i in range(3, 7):
         spread.start(i)
     own[0, 1].relay()
     length, label = r.got[0, 0, 1:2, 0:1], r.got[0, 0, 2:3, 0:1]
@@ -571,7 +579,7 @@
         gathers[ch].begin()
     for ch in range(2):
         r.first[ch * 64 : ch * 64 + 64] = first[ch]
-    for i in range(4):
+    for i in range(3):
         spread.arrive(i)
 
     def project(b):
@@ -581,41 +589,40 @@
 
     r.query_t[...] = (r.qkv[:, 0:128] * SCALE).T
     r.values_t[...] = r.qkv[:, 256:384].T
+    spread.arrive(3)
     r.out_t[...] = r.out_w[...].T
     seen = lax.broadcasted_iota(jnp.int32, (1024, 256), 0) < length
 
-    def attend(b):
+    def attend(b, head):
         cols = rows256(b)
-        for head in range(2):
-            scores = jnp.dot(
-                r.qkv[:, 128:256], of_head(r.query_t[:, cols], head, 0), preferred_element_type=F32
-            )
-            scores = jnp.where(seen, scores, -1e30)
-            expo = jnp.exp(scores - jnp.max(scores, axis=0, keepdims=True))
-            probs = (expo * (1.0 / jnp.sum(expo, axis=0, keepdims=True))).astype(BF16)
-            r.probs_t[head, :, cols] = probs
-            rows = slice(head * 64, head * 64 + 64)
-            r.context_t[rows, cols] = jnp.dot(
-                r.values_t[rows], probs, preferred_element_type=F32
-            ).astype(BF16)
+        scores = jnp.dot(r.qkv[:, 128:256], of_head(r.query_t[:, cols], head, 0), preferred_element_type=F32)
+        scores = jnp.where(seen, scores, -1e30)
+        expo = jnp.exp(scores - jnp.max(scores, axis=0, keepdims=True))
+        probs = (expo * (1.0 / jnp.sum(expo, axis=0, keepdims=True))).astype(BF16)
+        r.probs_t[head, :, cols] = probs
+        rows = slice(head * 64, head * 64 + 64)
+        r.context_t[rows, cols] = jnp.dot(r.values_t[rows], probs, preferred_element_type=F32).astype(BF16)
+
+    def put_out(b):
+        cols = rows256(b)
         r.terms[cols] = jnp.dot(r.context_t[:, cols].T, r.out_t[...], preferred_element_type=F32).astype(BF16)
 
     summed = PairOwner(r.terms, r, "a")
-    attend(op)
-    summed.push(0)
-    attend(up)
-    summed.push(1)
-    summed.pull(0)
-    for owner in summed.owners:
-        owner.begin()
-    attend(dn)
-    summed.push(2)
-    summed.pull(1)
-    attend(y)
-    summed.push(3)
-    summed.pull(2)
-    for owner in summed.owners:
-        owner.relay()
+    for i, b in enumerate(summed.order):
+        attend(b, 0)
+        if i > 0:
+            summed.pull(i - 1)
+            for owner in summed.owners:
+                if i == 1:
+                    owner.begin()
+                else:
+                    owner.early((i - 2,))
+        if i == 3:
+            summed.owners[0].relay()
+        attend(b, 1)
+        put_out(b)
+        summed.push(i)
+    summed.owners[1].relay()
     summed.pull(3)
     more = [Gather(r.normed_two, ch, r.a_asend.at[ch], r.a_arecv.at[ch]) for ch in range(2)]
     for ch in range(2):
@@ -694,6 +701,9 @@
         owner.begin()
     for i in range(1, 4):
         back.pull(i)
+        if i < 3:
+            for owner in back.owners:
+                owner.early((i - 1,))
     for block in range(4):
         cols = pl.ds(block * 256, 256)
         r.up_term[cols] = lax.dot_general(
@@ -719,34 +729,52 @@
     r.grad_k[...] = jnp.zeros((1024, 128), F32)
     r.grad_v[...] = jnp.zeros((1024, 128), F32)
 
-    def attend_back(b):
+    def back_values(b):
         cols = rows256(b)
         g_context = jnp.dot(r.g_second[cols], r.out_w[...], preferred_element_type=F32)
         g_context_t = g_context.T
         g_context = g_context.astype(BF16)
+        for head in range(2):
+            r.grad_v[...] += jnp.dot(
+                r.probs_t[head, :, cols], of_head(g_context, head, 1), preferred_element_type=F32
+            )
+        return g_context_t
+
+    def back_scores(b, g_context_t):
+        cols = rows256(b)
         product = g_context_t * r.context_t[:, cols].astype(F32)
         query = r.qkv[cols, 0:128] * SCALE
         for head in range(2):
             rows = slice(head * 64, head * 64 + 64)
-            probs = r.probs_t[head, :, cols]
             delta = jnp.sum(product[rows], axis=0, keepdims=True)
             moved = jnp.dot(
                 r.qkv[:, 256:384], of_head(g_context_t, head, 0).astype(BF16), preferred_element_type=F32
             )
-            g_scores = (probs.astype(F32) * (moved - delta)).astype(BF16)
+            g_scores = (r.probs_t[head, :, cols].astype(F32) * (moved - delta)).astype(BF16)
             r.grad_q[rows, cols] = jnp.dot(
                 r.keys_t[rows], g_scores, preferred_element_type=F32
             ).astype(BF16)
             r.grad_k[...] += jnp.dot(g_scores, of_head(query, head, 1), preferred_element_type=F32)
-            r.grad_v[...] += jnp.dot(probs, of_head(g_context, head, 1), preferred_element_type=F32)
-
-    gather_beside(last, attend_back)
-    r.out_term[...] = jnp.dot(r.context_t[...], r.g_second[...], preferred_element_type=F32).T.astype(BF16)
-    collect.start(2)
-    for piece in range(3):
-        left = r.grad_q[...] if piece == 0 else (r.grad_k, r.grad_v)[piece - 1][...].T.astype(BF16)
+
+    def send_term(piece, left):
         r.qkv_term[piece] = jnp.dot(left, r.normed[...], preferred_element_type=F32).T.astype(BF16)
         collect.start(3 + piece)
+
+    def attend_back(b):
+        back_scores(b, back_values(b))
+
+    def attend_back_last(b):
+        r.out_term[...] = jnp.dot(
+            r.context_t[...], r.g_second[...], preferred_element_type=F32
+        ).T.astype(BF16)
+        collect.start(2)
+        g_context_t = back_values(b)
+        send_term(2, r.grad_v[...].T.astype(BF16))
+        back_scores(b, g_context_t)
+        send_term(0, r.grad_q[...])
+        send_term(1, r.grad_k[...].T.astype(BF16))
+
+    gather_beside(last, attend_back, attend_back_last)
 
     collect.arrive(0)
     begin = ((me["xl"] * 4 + me["z"]) * 2 + me["c"]) * 64
@@ -810,11 +838,11 @@
         shard=vm((padded, 1024), BF16),
         chosen=vm((256, padded), BF16),
         rows=vm((2, 2, 4, 64, 1024), BF16),
-        e_stage=vm((2, 2, 2, 64, 1024), BF16),
+        e_stage=vm((2, 2, 2, 32, 1024), BF16),
         e_far=vm((2, 2, 2, 32, 1024), BF16),
         e_near=vm((2, 2, 2, 64, 1024), BF16),
-        e_rsend=dma((2, 2, 4)),
-        e_rrecv=dma((2, 2, 4)),
+        e_rsend=dma((2, 2, 6)),
+        e_rrecv=dma((2, 2, 6)),
         e_asend=dma((2, 9)),
         e_arecv=dma((2, 9)),
         total=vm((2, 64, 1024), BF16),
@@ -864,7 +892,7 @@
         in_specs=list(inputs.values()),
         out_specs=[VM] * len(outputs),
         scratch_shapes=list(scratch.values()),
-        compiler_params=params(1, 61),
+        compiler_params=params(1, 54),
         name="step",
     )(count, label, ids, table, qkv_s, out_s, up_s, down_s, head_s)
 

time: 137 us -> 135 us (0.985)
  Pallas kernels: 129 us -> 126 us
    pallas_call x1, Pallas kernels: 128 us -> 125 us  [step(): pl.pallas_call(functools.partial(step_kernel, (*inputs, *outputs, *scratc...]
where the time goes in v1:
time: 135 us
  Pallas kernels  126 us (93%)
  local copies, waits for them, and re-layouts  4.64 us (3%)
  between operations  3.71 us (3%)
    pallas_call x1, Pallas kernels, step(): pl.pallas_call(functools.partial(step_kernel, (*inputs, *outputs, *scratc...  125 us
    unnamed x10, local copies, waits for them, and re-layouts  4.64 us

profile of v1, /device:TPU:1, one launch (start us, length us, event | category | flops | bytes accessed | tf_op | source)
XLA Modules:
  0.0 134.6 jit_solution(3612271617005166431)
XLA Ops:
  1.9 125.4 %step.1 = (f32[64,512]{1,0:T(8,128)}, f32[64,512]{1,0:T(8,128)}, f32[64,128]{1,0:T(8,128)}, f32[1,128]{1,0:T(1,128)}, bf16[16,64,128]{2,1,0:T(8,128)(2,1)}, /*index=5*/bf16[3,16,64,128]{3,2,1,0:T(8,128)(2,1)}) custom-call(s32[1]{0:T(128)S(6)} %copy.16.refs_0_, s32[1]{0:T(128)S(6)} %copy.17.refs_1_, s32[1,128]{1,0:T(1,128)} %refs_2_.1, ...), custom_call_target="tpu_custom_call" | custom-call | tf_op jit(solution)/shard_map/step/pallas_call | solution.py:889
  127.3 0.0 copy-start
  127.3 1.1 copy-done
  128.5 0.0 copy-start.1
  128.5 0.9 copy-done.1
  129.4 0.0 copy-start.2
  129.4 0.9 copy-done.2
  130.3 0.0 copy-start.3
  130.3 0.9 copy-done.3
  131.2 0.0 copy-start.4
  131.2 0.8 copy-done.4
  132.0 0.8 results.1
Async XLA Ops:
  127.3 1.1 copy-start
  128.5 0.9 copy-start.1
  129.4 0.9 copy-start.2
  130.3 0.9 copy-start.3
  131.2 0.8 copy-start.4

commit v2 on v1

--- a/solution.py
+++ b/solution.py
@@ -363,13 +363,15 @@
             step.wait_send()
 
 
-def gather_beside(gathers, block_work, last_work=None):
+def gather_beside(gathers, block_work, last_work=None, after_sides=None):
     _, y, c, up, dn, op, oc = ring_places()
     for g in gathers:
         g.pair_own()
     block_work(y)
     for g in gathers:
         g.sides()
+    if after_sides is not None:
+        after_sides()
     for g in gathers:
         g.pair_sides()
     block_work(up)
@@ -585,12 +587,18 @@
     def project(b):
         r.qkv[rows256(b)] = jnp.dot(r.normed[rows256(b)], r.qkv_w[...], preferred_element_type=F32).astype(BF16)
 
-    gather_beside(gathers, project)
+    wide = [Gather(r.out_full, ch, r.wsend.at[ch], r.wrecv.at[ch]) for ch in range(2)]
+
+    def widen():
+        spread.arrive(3)
+        r.out_full[pl.ds(pl.multiple_of(slot * 128, 128), 128)] = r.out_w[...].T
+        for g in wide:
+            g.begin()
+
+    gather_beside(gathers, project, after_sides=widen)
 
     r.query_t[...] = (r.qkv[:, 0:128] * SCALE).T
     r.values_t[...] = r.qkv[:, 256:384].T
-    spread.arrive(3)
-    r.out_t[...] = r.out_w[...].T
     seen = lax.broadcasted_iota(jnp.int32, (1024, 256), 0) < length
 
     def attend(b, head):
@@ -603,30 +611,53 @@
         rows = slice(head * 64, head * 64 + 64)
         r.context_t[rows, cols] = jnp.dot(r.values_t[rows], probs, preferred_element_type=F32).astype(BF16)
 
-    def put_out(b):
-        cols = rows256(b)
-        r.terms[cols] = jnp.dot(r.context_t[:, cols].T, r.out_t[...], preferred_element_type=F32).astype(BF16)
-
-    summed = PairOwner(r.terms, r, "a")
-    for i, b in enumerate(summed.order):
+    order = (op, up, dn, y)
+    here128 = pl.ds(pl.multiple_of(slot * 128, 128), 128)
+
+    def piece(i, e):
+        return r.context.at[pl.ds(pl.multiple_of((order[i] * 2 + add_mod(c, e, 2)) * 128, 128), 128)]
+
+    pieces = {
+        (i, e): remote(
+            piece(i, e),
+            r.context_own.at[:, here128],
+            r.tsend.at[i, e],
+            r.trecv.at[i, e],
+            dict(y=order[i], c=add_mod(c, e, 2)),
+        )
+        for i in range(4)
+        for e in range(2)
+        if (i, e) != (3, 0)
+    }
+
+    def hand_over(i):
+        r.context[rows256(order[i])] = r.context_t[:, rows256(order[i])].T
+        for e in range(2):
+            if (i, e) in pieces:
+                pieces[i, e].start()
+            else:
+                r.context_own[:, here128] = r.context[here128]
+
+    for i, b in enumerate(order):
         attend(b, 0)
-        if i > 0:
-            summed.pull(i - 1)
-            for owner in summed.owners:
-                if i == 1:
-                    owner.begin()
-                else:
-                    owner.early((i - 2,))
-        if i == 3:
-            summed.owners[0].relay()
         attend(b, 1)
-        put_out(b)
-        summed.push(i)
-    summed.owners[1].relay()
-    summed.pull(3)
+        hand_over(i)
+        if i == 1:
+            for g in wide:
+                g.sides()
+        if i == 2:
+            for g in wide:
+                g.far()
+    for step in pieces.values():
+        step.wait_recv()
+    for g in wide:
+        g.pair_own()
+        g.pair_sides()
+        g.pair_far()
+    attn = jnp.dot(r.context_own[...], r.out_full[...], preferred_element_type=F32)
     more = [Gather(r.normed_two, ch, r.a_asend.at[ch], r.a_arecv.at[ch]) for ch in range(2)]
     for ch in range(2):
-        second = (r.first[ch * 64 : ch * 64 + 64] + summed.owners[ch].finish()).astype(BF16)
+        second = (r.first[ch * 64 : ch * 64 + 64] + attn[ch * 64 : ch * 64 + 64]).astype(BF16)
         r.second[ch * 64 : ch * 64 + 64] = second
         r.normed_two[own_rows(ch)] = normalize(second.astype(F32)).astype(BF16)
         more[ch].begin()
@@ -796,9 +827,10 @@
         owner.sent()
     for step in cross:
         step.wait_send()
-    for g in gathers + more + last:
+    for g in gathers + wide + more + last:
         g.sent()
-    summed.sent()
+    for step in pieces.values():
+        step.wait_send()
     back.sent()
     for i in range(6):
         collect.sent(i)
@@ -860,11 +892,17 @@
         query_t=vm((128, 1024), BF16),
         values_t=vm((128, 1024), BF16),
         keys_t=vm((128, 1024), BF16),
-        out_t=vm((128, 1024), BF16),
+        out_full=vm((1024, 1024), BF16),
+        wsend=dma((2, 9)),
+        wrecv=dma((2, 9)),
+        context=vm((1024, 128), BF16),
+        context_own=vm((128, 1024), BF16),
+        tsend=dma((4, 2)),
+        trecv=dma((4, 2)),
+        a_asend=dma((2, 9)),
+        a_arecv=dma((2, 9)),
         probs_t=vm((2, 1024, 1024), BF16),
         context_t=vm((128, 1024), BF16),
-        terms=vm((1024, 1024), BF16),
-        **pair_owner_scratch("a"),
         second=vm((128, 1024), BF16),
         normed_two=vm((1024, 1024), BF16),
         hidden_sum=vm((1, 512), F32),
@@ -897,13 +935,20 @@
     )(count, label, ids, table, qkv_s, out_s, up_s, down_s, head_s)
 
 
-def results_kernel(up, down, head, out_buf, qkv_buf, up_grad, down_grad, head_grad, out_grad, qkv_grad):
-    up_grad[...] = up[...]
-    down_grad[...] = down[...]
-    head_grad[...] = head[...]
-    out_grad[...] = total_of(out_buf)
-    for i in range(3):
-        qkv_grad[i] = total_of(qkv_buf.at[i])
+def results_kernel(*refs):
+    sources, targets, here, sems = refs[:5], refs[5:10], refs[10:15], refs[15]
+    steps = [pltpu.make_async_copy(sources[i], here[i], sems.at[i]) for i in range(5)]
+    for step in steps:
+        step.start()
+    for i in range(5):
+        steps[i].wait()
+        if i < 3:
+            targets[i][...] = here[i][...]
+        elif i == 3:
+            targets[i][...] = total_of(here[i])
+        else:
+            for piece in range(3):
+                targets[i][piece] = total_of(here[i].at[piece])
 
 
 def results(*arrays):
@@ -916,9 +961,10 @@
             jax.ShapeDtypeStruct((64, 128), F32),
             jax.ShapeDtypeStruct((3, 64, 128), F32),
         ],
-        in_specs=[VM] * 5,
+        in_specs=[HBM] * 5,
         out_specs=[VM] * 5,
-        compiler_params=pltpu.CompilerParams(vmem_limit_bytes=8 * 2**20),
+        scratch_shapes=[pltpu.VMEM(a.shape, a.dtype) for a in arrays] + [pltpu.SemaphoreType.DMA((5,))],
+        compiler_params=pltpu.CompilerParams(vmem_limit_bytes=67043328),
         name="results",
     )(*arrays)
 

time: 135 us -> 131 us (0.970)
  local copies, waits for them, and re-layouts: 4.64 us -> 0 us
    unnamed x10 -> x0, local copies, waits for them, and re-layouts: 4.64 us -> none
    pallas_call x1, Pallas kernels: 0.81 us -> 2.17 us  [results(): pl.pallas_call(results_kernel, out_shape=[jax.ShapeDtypeStruct((64, 512),...]
where the time goes in v2:
time: 131 us
  Pallas kernels  127 us (97%)
  between operations  3.7 us (3%)
    pallas_call x1, Pallas kernels, step(): pl.pallas_call(functools.partial(step_kernel, (*inputs, *outputs, *scratc...  125 us

profile of v2, /device:TPU:1, one launch (start us, length us, event | category | flops | bytes accessed | tf_op | source)
XLA Modules:
  0.0 130.6 jit_solution(13857576900932483344)
XLA Ops:
  1.9 124.7 %step.1 = (f32[64,512]{1,0:T(8,128)}, f32[64,512]{1,0:T(8,128)}, f32[64,128]{1,0:T(8,128)}, f32[1,128]{1,0:T(1,128)}, bf16[16,64,128]{2,1,0:T(8,128)(2,1)}, /*index=5*/bf16[3,16,64,128]{3,2,1,0:T(8,128)(2,1)}) custom-call(s32[1]{0:T(128)S(6)} %copy.16.refs_0_, s32[1]{0:T(128)S(6)} %copy.17.refs_1_, s32[1,128]{1,0:T(1,128)} %refs_2_.1, ...), custom_call_target="tpu_custom_call" | custom-call | tf_op jit(solution)/shard_map/step/pallas_call | solution.py:927
  126.7 2.2 %results.1 = (f32[64,512]{1,0:T(8,128)}, f32[64,512]{1,0:T(8,128)}, f32[64,128]{1,0:T(8,128)}, f32[64,128]{1,0:T(8,128)}, f32[3,64,128]{2,1,0:T(8,128)}) custom-call(f32[64,512]{1,0:T(8,128)} %get-tuple-element.18.refs_0_, f32[64,512]{1,0:T(8,128)} %get-tuple-element.19.refs_1_, f32[64,128]{1,0:T(8,128)} %get-tuple-element.20.refs_2_, ...), custom_call_target="tpu_custom_call" | custom-call | tf_op jit(solution)/shard_map/results/pallas_call | solution.py:955

commit v3 on v2

--- a/solution.py
+++ b/solution.py
@@ -642,12 +642,11 @@
         attend(b, 0)
         attend(b, 1)
         hand_over(i)
-        if i == 1:
+        if i == 0:
             for g in wide:
                 g.sides()
-        if i == 2:
-            for g in wide:
-                g.far()
+    for g in wide:
+        g.far()
     for step in pieces.values():
         step.wait_recv()
     for g in wide:
@@ -727,9 +726,10 @@
             grad, r.up_w[...], RHS_T, preferred_element_type=F32
         ).astype(BF16)
         back.push(i)
-    back.pull(0)
-    for owner in back.owners:
-        owner.begin()
+        if i == 2:
+            back.pull(0)
+            for owner in back.owners:
+                owner.begin()
     for i in range(1, 4):
         back.pull(i)
         if i < 3:

time: 131 us -> 128 us (0.977)
  Pallas kernels: 127 us -> 124 us
    pallas_call x1, Pallas kernels: 125 us -> 122 us  [step(): pl.pallas_call(functools.partial(step_kernel, (*inputs, *outputs, *scratc...]
where the time goes in v3:
time: 128 us
  Pallas kernels  124 us (97%)
  between operations  3.7 us (3%)
    pallas_call x1, Pallas kernels, step(): pl.pallas_call(functools.partial(step_kernel, (*inputs, *outputs, *scratc...  122 us

profile of v3, /device:TPU:1, one launch (start us, length us, event | category | flops | bytes accessed | tf_op | source)
XLA Modules:
  0.0 127.7 jit_solution(7519231752289033454)
XLA Ops:
  1.9 121.9 %step.1 = (f32[64,512]{1,0:T(8,128)}, f32[64,512]{1,0:T(8,128)}, f32[64,128]{1,0:T(8,128)}, f32[1,128]{1,0:T(1,128)}, bf16[16,64,128]{2,1,0:T(8,128)(2,1)}, /*index=5*/bf16[3,16,64,128]{3,2,1,0:T(8,128)(2,1)}) custom-call(s32[1]{0:T(128)S(6)} %copy.16.refs_0_, s32[1]{0:T(128)S(6)} %copy.17.refs_1_, s32[1,128]{1,0:T(1,128)} %refs_2_.1, ...), custom_call_target="tpu_custom_call" | custom-call | tf_op jit(solution)/shard_map/step/pallas_call | solution.py:927
  123.8 2.2 %results.1 = (f32[64,512]{1,0:T(8,128)}, f32[64,512]{1,0:T(8,128)}, f32[64,128]{1,0:T(8,128)}, f32[64,128]{1,0:T(8,128)}, f32[3,64,128]{2,1,0:T(8,128)}) custom-call(f32[64,512]{1,0:T(8,128)} %get-tuple-element.18.refs_0_, f32[64,512]{1,0:T(8,128)} %get-tuple-element.19.refs_1_, f32[64,128]{1,0:T(8,128)} %get-tuple-element.20.refs_2_, ...), custom_call_target="tpu_custom_call" | custom-call | tf_op jit(solution)/shard_map/results/pallas_call | solution.py:955

commit v4 on v3

--- a/solution.py
+++ b/solution.py
@@ -194,6 +194,107 @@
                     ).start()
             else:
                 copy(a, k, e).start()
+
+
+    def across(self, x):
+        x = lax.rem(x, 4)
+        high = jnp.where(x >= 2, 1, 0)
+        return dict(xh=high, xl=x - 2 * high)
+
+    def greet_relays(self):
+        me = self.me
+        xl, z, c, xh, y = me["xl"], me["z"], me["c"], me["xh"], me["y"]
+        way = 1 - 2 * c
+        behind = add_mod(z, 4 - way, 4)
+        signal(dict(xl=xl, xh=xh, z=behind, c=xh, y=y))
+        for high in range(2):
+            signal(dict(xl=1 - xl, xh=high, z=behind, c=xh, y=y))
+        ends = self.across(2 * xh + xl + 4 + way)
+        for k in (0, 1, 3, 2):
+            place = behind if k == 2 else add_mod(z, 4 - k, 4)
+            signal(dict(xl=ends["xl"], xh=1 - ends["xh"], z=place, c=ends["xh"], y=y))
+        before = self.across(2 * xh + xl + 4 - way)
+        signal(dict(z=behind))
+        signal(dict(z=z, **before))
+        signal(dict(z=behind, **before))
+        return jnp.where(self.here, 4, 10) + 3
+
+    def start_relayed(self, i, j, buf, arrive):
+        me = self.me
+        xl, z, c, xh, y = me["xl"], me["z"], me["c"], me["xh"], me["y"]
+        block, place = self.items[i][:2]
+
+        def send(number, target, recv, device):
+            remote(block(number), target, self.send.at[i], recv, device).start()
+
+        for a, k in ((0, 2), (1, 2), (0, 1), (0, 3), (0, 0), (1, 1), (1, 3), (1, 0)):
+            for e in range(2):
+                way = 1 - 2 * e
+                number = self.number(a, k, e)
+                hop = 2 - way if k == 2 else k
+
+                def direct(a=a, k=k, e=e, number=number):
+                    send(number, place(self.slot), self.recv.at[i], self.target(a, k, e))
+
+                def on_z(index, a=a, e=e, number=number, hop=hop):
+                    device = dict(xl=add_mod(xl, a, 2), xh=c, z=add_mod(z, hop, 4), c=e, y=y)
+                    send(number, buf.at[j, index], arrive.at[j, index], device)
+
+                def on_x(index, e=e, number=number, hop=hop, way=way):
+                    device = dict(z=add_mod(z, hop, 4), c=e, y=y, **self.across(2 * c + xl + 4 - way))
+                    send(number, buf.at[j, index], arrive.at[j, index], device)
+
+                if a == 1:
+                    if k == 2:
+                        on_z(1 + xh)
+                    else:
+                        direct()
+                    continue
+
+                @pl.when(jnp.logical_not(self.here))
+                def _(k=k, on_x=on_x):
+                    on_x({0: 3, 1: 4, 3: 5, 2: 6}[k])
+
+                if k == 2:
+
+                    @pl.when(self.here)
+                    def _(on_z=on_z):
+                        on_z(0)
+                elif k:
+
+                    @pl.when(self.here)
+                    def _(direct=direct):
+                        direct()
+                else:
+                    is_self = jnp.logical_and(self.here, e == self.other)
+
+                    @pl.when(jnp.logical_and(self.here, e != self.other))
+                    def _(direct=direct):
+                        direct()
+
+                    @pl.when(is_self)
+                    def _(number=number):
+                        pltpu.make_async_copy(block(number), place(self.slot), self.recv.at[i]).start()
+
+    def forward(self, i, j, buf, arrive, leave):
+        me = self.me
+        xl, z, c, xh = me["xl"], me["z"], me["c"], me["xh"]
+        place = self.items[i][1]
+        way = 1 - 2 * c
+        behind, ahead = add_mod(z, 4 - way, 4), add_mod(z, 4 + way, 4)
+        ends = self.across(2 * xh + xl + 4 + way)
+
+        def go(index, slot, device):
+            pltpu.make_async_copy(buf.at[j, index], buf.at[j, index], arrive.at[j, index]).wait()
+            remote(buf.at[j, index], place(slot), leave.at[j], self.recv.at[i], device).start()
+
+        go(0, (xl * 4 + behind) * 2 + xh, dict(z=ahead))
+        for high in range(2):
+            go(1 + high, ((1 - xl) * 4 + behind) * 2 + high, dict(z=ahead))
+        for index, k in ((6, 2), (4, 1), (5, 3), (3, 0)):
+            source = behind if k == 2 else add_mod(z, 4 - k, 4)
+            slot = (ends["xl"] * 4 + source) * 2 + 1 - ends["xh"]
+            go(index, slot, dict(z=ahead if k == 2 else z, **ends))
 
     def arrive(self, i):
         whole = self.items[i][2]
@@ -497,7 +598,7 @@
         signal(device)
     for k, e in peers:
         signal(dict(y=add_mod(y, (4 - k) % 4, 4), c=add_mod(c, e, 2)))
-    greeted = tokens.greet() + spread.greet() + collect.greet() + 11
+    greeted = tokens.greet() + spread.greet() + collect.greet() + collect.greet_relays() + 11
     if padded > vocab:
         r.shard[vocab:padded] = jnp.zeros((padded - vocab, 1024), BF16)
     fetch_ids.wait()
@@ -789,7 +890,10 @@
 
     def send_term(piece, left):
         r.qkv_term[piece] = jnp.dot(left, r.normed[...], preferred_element_type=F32).T.astype(BF16)
-        collect.start(3 + piece)
+        collect.start_relayed(3 + piece, 1 + piece, r.relay_buf, r.relay_in)
+
+    def pass_on(j):
+        collect.forward(2 + j, j, r.relay_buf, r.relay_in, r.relay_out)
 
     def attend_back(b):
         back_scores(b, back_values(b))
@@ -798,12 +902,14 @@
         r.out_term[...] = jnp.dot(
             r.context_t[...], r.g_second[...], preferred_element_type=F32
         ).T.astype(BF16)
-        collect.start(2)
+        collect.start_relayed(2, 0, r.relay_buf, r.relay_in)
         g_context_t = back_values(b)
         send_term(2, r.grad_v[...].T.astype(BF16))
         back_scores(b, g_context_t)
         send_term(0, r.grad_q[...])
+        pass_on(0)
         send_term(1, r.grad_k[...].T.astype(BF16))
+        pass_on(3)
 
     gather_beside(last, attend_back, attend_back_last)
 
@@ -817,6 +923,8 @@
         picked(packets[:, 1536:2560], begin), packets[:, 2560:2688], precision=HIGH, preferred_element_type=F32
     )
     r.loss[...] = jnp.sum(packets[:, 2688:2816], axis=0, keepdims=True) / 16.0
+    pass_on(1)
+    pass_on(2)
     collect.arrive(1)
     r.up_grad[...] = total_of(r.up_buf)
 
@@ -834,6 +942,8 @@
     back.sent()
     for i in range(6):
         collect.sent(i)
+    for j in range(4):
+        pltpu.make_async_copy(r.relay_buf.at[j], r.relay_buf.at[j], r.relay_out.at[j]).wait()
     for i in range(2, 6):
         collect.arrive(i)
 
@@ -867,6 +977,9 @@
         srecv=dma((7,)),
         csend=dma((6,)),
         crecv=dma((6,)),
+        relay_buf=vm((4, 7, 64, 128), BF16),
+        relay_in=dma((4, 7)),
+        relay_out=dma((4,)),
         shard=vm((padded, 1024), BF16),
         chosen=vm((256, padded), BF16),
         rows=vm((2, 2, 4, 64, 1024), BF16),

time: 128 us -> 129 us (level)
  no operation moved by 1% of the time
where the time goes in v4:
time: 129 us
  Pallas kernels  125 us (97%)
  between operations  3.7 us (3%)
    pallas_call x1, Pallas kernels, step(): pl.pallas_call(functools.partial(step_kernel, (*inputs, *outputs, *scratc...  123 us

profile of v4, /device:TPU:1, one launch (start us, length us, event | category | flops | bytes accessed | tf_op | source)
XLA Modules:
  0.0 128.9 jit_solution(2481282271538006655)
XLA Ops:
  1.9 123.0 %step.1 = (f32[64,512]{1,0:T(8,128)}, f32[64,512]{1,0:T(8,128)}, f32[64,128]{1,0:T(8,128)}, f32[1,128]{1,0:T(1,128)}, bf16[16,64,128]{2,1,0:T(8,128)(2,1)}, /*index=5*/bf16[3,16,64,128]{3,2,1,0:T(8,128)(2,1)}) custom-call(s32[1]{0:T(128)S(6)} %copy.16.refs_0_, s32[1]{0:T(128)S(6)} %copy.17.refs_1_, s32[1,128]{1,0:T(1,128)} %refs_2_.1, ...), custom_call_target="tpu_custom_call" | custom-call | tf_op jit(solution)/shard_map/step/pallas_call | solution.py:1040
  125.0 2.2 %results.1 = (f32[64,512]{1,0:T(8,128)}, f32[64,512]{1,0:T(8,128)}, f32[64,128]{1,0:T(8,128)}, f32[64,128]{1,0:T(8,128)}, f32[3,64,128]{2,1,0:T(8,128)}) custom-call(f32[64,512]{1,0:T(8,128)} %get-tuple-element.18.refs_0_, f32[64,512]{1,0:T(8,128)} %get-tuple-element.19.refs_1_, f32[64,128]{1,0:T(8,128)} %get-tuple-element.20.refs_2_, ...), custom_call_target="tpu_custom_call" | custom-call | tf_op jit(solution)/shard_map/results/pallas_call | solution.py:1068

commit v5 on v3

--- a/solution.py
+++ b/solution.py
@@ -562,8 +562,7 @@
     own[0, 0].relay()
     r.total[1] = own[1, 1].finish().astype(BF16)
     cross[1].start()
-    for i in range(3, 7):
-        spread.start(i)
+    spread.start(3)
     own[0, 1].relay()
     length, label = r.got[0, 0, 1:2, 0:1], r.got[0, 0, 2:3, 0:1]
     gathers = [Gather(r.normed, ch, r.e_asend.at[ch], r.e_arecv.at[ch]) for ch in range(2)]
@@ -579,6 +578,8 @@
         first.append(value)
         r.normed[own_rows(ch)] = normalize(value).astype(BF16)
         gathers[ch].begin()
+    for i in range(4, 7):
+        spread.start(i)
     for ch in range(2):
         r.first[ch * 64 : ch * 64 + 64] = first[ch]
     for i in range(3):
@@ -834,8 +835,11 @@
     back.sent()
     for i in range(6):
         collect.sent(i)
-    for i in range(2, 6):
-        collect.arrive(i)
+    collect.arrive(2)
+    r.out_grad[...] = total_of(r.out_buf)
+    for piece in (2, 0, 1):
+        collect.arrive(3 + piece)
+        r.qkv_grad[piece] = total_of(r.qkv_buf.at[piece])
 
 
 HBM = pl.BlockSpec(memory_space=pltpu.HBM)
@@ -851,8 +855,8 @@
         down_grad=jax.ShapeDtypeStruct((64, 512), F32),
         head_grad=jax.ShapeDtypeStruct((64, 128), F32),
         loss=jax.ShapeDtypeStruct((1, 128), F32),
-        out_buf=jax.ShapeDtypeStruct((16, 64, 128), BF16),
-        qkv_buf=jax.ShapeDtypeStruct((3, 16, 64, 128), BF16),
+        out_grad=jax.ShapeDtypeStruct((64, 128), F32),
+        qkv_grad=jax.ShapeDtypeStruct((3, 64, 128), F32),
     )
     dma = pltpu.SemaphoreType.DMA
     vm = pltpu.VMEM
@@ -923,6 +927,8 @@
         grad_v=vm((1024, 128), F32),
         out_term=vm((1024, 128), BF16),
         qkv_term=vm((3, 1024, 128), BF16),
+        out_buf=vm((16, 64, 128), BF16),
+        qkv_buf=vm((3, 16, 64, 128), BF16),
     )
     return pl.pallas_call(
         functools.partial(step_kernel, (*inputs, *outputs, *scratch)),
@@ -942,13 +948,7 @@
         step.start()
     for i in range(5):
         steps[i].wait()
-        if i < 3:
-            targets[i][...] = here[i][...]
-        elif i == 3:
-            targets[i][...] = total_of(here[i])
-        else:
-            for piece in range(3):
-                targets[i][piece] = total_of(here[i].at[piece])
+        targets[i][...] = here[i][...]
 
 
 def results(*arrays):
@@ -970,7 +970,7 @@
 
 
 def per_device(token_ids, lengths, teacher_bins, table, qkv_shard, out_shard, up_shard, down_shard, head_shard):
-    up_grad, down_grad, head_grad, loss, out_buf, qkv_buf = step(
+    up_grad, down_grad, head_grad, loss, out_grad, qkv_grad = step(
         lengths,
         teacher_bins,
         token_ids,
@@ -981,7 +981,7 @@
         down_shard.T,
         head_shard,
     )
-    up_grad, down_grad, head_grad, out_grad, qkv_grad = results(up_grad, down_grad, head_grad, out_buf, qkv_buf)
+    up_grad, down_grad, head_grad, out_grad, qkv_grad = results(up_grad, down_grad, head_grad, out_grad, qkv_grad)
     return loss[0, 0], jnp.transpose(qkv_grad, (1, 0, 2)), out_grad.T, up_grad, down_grad.T, head_grad
 
 

time: 128 us -> 127 us (level)
  no operation moved by 1% of the time
where the time goes in v5:
time: 127 us
  Pallas kernels  123 us (97%)
  between operations  3.74 us (3%)
    pallas_call x1, Pallas kernels, step(): pl.pallas_call(functools.partial(step_kernel, (*inputs, *outputs, *scratc...  121 us

profile of v5, /device:TPU:1, one launch (start us, length us, event | category | flops | bytes accessed | tf_op | source)
XLA Modules:
  0.0 127.1 jit_solution(8348569209385979369)
XLA Ops:
  1.9 121.5 %step.1 = (f32[64,512]{1,0:T(8,128)}, f32[64,512]{1,0:T(8,128)}, f32[64,128]{1,0:T(8,128)}, f32[1,128]{1,0:T(1,128)}, f32[64,128]{1,0:T(8,128)}, /*index=5*/f32[3,64,128]{2,1,0:T(8,128)}) custom-call(s32[1]{0:T(128)S(6)} %copy.16.refs_0_, s32[1]{0:T(128)S(6)} %copy.17.refs_1_, s32[1,128]{1,0:T(1,128)} %refs_2_.1, bf16[3816,1024]{1,0:T(8,128)(2,1)} %refs_3_.1, ...), custom_call_target="tpu_custom_call" | custom-call | tf_op jit(solution)/shard_map/step/pallas_call | solution.py:933
  123.4 1.8 %results.1 = (f32[64,512]{1,0:T(8,128)}, f32[64,512]{1,0:T(8,128)}, f32[64,128]{1,0:T(8,128)}, f32[64,128]{1,0:T(8,128)}, f32[3,64,128]{2,1,0:T(8,128)}) custom-call(f32[64,512]{1,0:T(8,128)} %get-tuple-element.18.refs_0_, f32[64,512]{1,0:T(8,128)} %get-tuple-element.19.refs_1_, f32[64,128]{1,0:T(8,128)} %get-tuple-element.20.refs_2_, ...), custom_call_target="tpu_custom_call" | custom-call | tf_op jit(solution)/shard_map/results/pallas_call | solution.py:955

commit v6 on v5

--- a/solution.py
+++ b/solution.py
@@ -641,13 +641,14 @@
 
     for i, b in enumerate(order):
         attend(b, 0)
+        if i == 3:
+            wide[0].far()
         attend(b, 1)
         hand_over(i)
         if i == 0:
             for g in wide:
                 g.sides()
-    for g in wide:
-        g.far()
+    wide[1].far()
     for step in pieces.values():
         step.wait_recv()
     for g in wide:

time: 127 us -> 127 us (level)
  no operation moved by 1% of the time
where the time goes in v6:
time: 127 us
  Pallas kernels  123 us (97%)
  between operations  3.74 us (3%)
    pallas_call x1, Pallas kernels, step(): pl.pallas_call(functools.partial(step_kernel, (*inputs, *outputs, *scratc...  121 us

profile of v6, /device:TPU:1, one launch (start us, length us, event | category | flops | bytes accessed | tf_op | source)
XLA Modules:
  0.0 127.1 jit_solution(14432763672720644563)
XLA Ops:
  1.9 121.5 %step.1 = (f32[64,512]{1,0:T(8,128)}, f32[64,512]{1,0:T(8,128)}, f32[64,128]{1,0:T(8,128)}, f32[1,128]{1,0:T(1,128)}, f32[64,128]{1,0:T(8,128)}, /*index=5*/f32[3,64,128]{2,1,0:T(8,128)}) custom-call(s32[1]{0:T(128)S(6)} %copy.16.refs_0_, s32[1]{0:T(128)S(6)} %copy.17.refs_1_, s32[1,128]{1,0:T(1,128)} %refs_2_.1, bf16[3816,1024]{1,0:T(8,128)(2,1)} %refs_3_.1, ...), custom_call_target="tpu_custom_call" | custom-call | tf_op jit(solution)/shard_map/step/pallas_call | solution.py:934
  123.4 1.8 %results.1 = (f32[64,512]{1,0:T(8,128)}, f32[64,512]{1,0:T(8,128)}, f32[64,128]{1,0:T(8,128)}, f32[64,128]{1,0:T(8,128)}, f32[3,64,128]{2,1,0:T(8,128)}) custom-call(f32[64,512]{1,0:T(8,128)} %get-tuple-element.18.refs_0_, f32[64,512]{1,0:T(8,128)} %get-tuple-element.19.refs_1_, f32[64,128]{1,0:T(8,128)} %get-tuple-element.20.refs_2_, ...), custom_call_target="tpu_custom_call" | custom-call | tf_op jit(solution)/shard_map/results/pallas_call | solution.py:956
